TPU v7x, 32 devices: a whole 2x2x4 slice. The times are simulated.
32 devices in a mesh: band: 8 (over z, x), space: 4 (over y, core).
Axes of the slice: x: 2, y: 2, z: 4, core: 2. Of those that a mesh axis runs over, the one named last changes fastest.
Arguments:
- orbitals: bfloat16 [64, 64, 160, 128], P('band', None, 'space'), may hold values from -8.5 to 8.5
- occupations: float32 [64], P('band'), may hold values from 0.07 to 2.5
Outputs:
- potential: float32 [64, 160, 128], P('band', 'space')
All inputs are finite; a program needn't handle non-finite values.
Results may differ from a plain program's by a relative error of at most 0.0003.
Values sent between devices are 32-bit elements; how exact they have to be, the bound alone decides.
A program may use at most 64 MiB of HBM per device.

v0:
```python
import math
import jax
import jax.numpy as jnp
from jax import lax
from jax.sharding import PartitionSpec as P

ITERS = 3
four_pi = 4.0 * math.pi


def with_halo(shard, sides, width):
    for axis, dim in sides:
        peers, length = (lax.axis_size(axis), shard.shape[dim])
        up = [(i, (i + 1) % peers) for i in range(peers - 1)]
        down = [(j, i) for i, j in up]
        last = lax.slice_in_dim(shard, length - width, length, axis=dim)
        first = lax.slice_in_dim(shard, 0, width, axis=dim)
        before = lax.ppermute(last, axis, up)
        after = lax.ppermute(first, axis, down)
        shard = jnp.concatenate([before, shard, after], axis=dim)
    return shard


def stencil(padded):
    center = padded[2:-2, 2:-2, 2:-2]
    near = padded[3:-1, 2:-2, 2:-2] + padded[1:-3, 2:-2, 2:-2]
    near = near + padded[2:-2, 3:-1, 2:-2] + padded[2:-2, 1:-3, 2:-2]
    near = near + padded[2:-2, 2:-2, 3:-1] + padded[2:-2, 2:-2, 1:-3]
    distant = padded[4:, 2:-2, 2:-2] + padded[:-4, 2:-2, 2:-2]
    distant = distant + padded[2:-2, 4:, 2:-2] + padded[2:-2, :-4, 2:-2]
    distant = distant + padded[2:-2, 2:-2, 4:] + padded[2:-2, 2:-2, :-4]
    return 7.5 * center - 4.0 / 3.0 * near + 1.0 / 12.0 * distant


def operate(field):
    widened = with_halo(field, (("band", 0), ("space", 1)), 2)
    return stencil(jnp.pad(widened, ((0, 0), (0, 0), (2, 2))))


def paired_sums(residual, image):
    return lax.psum((jnp.sum(residual * residual), jnp.sum(residual * image)), ("band", "space"))


def local(orbitals, occupations):

    def accumulate(index, total):
        wave = lax.dynamic_index_in_dim(orbitals, index, 0, keepdims=False).astype(jnp.float32)
        return total + occupations[index] * wave * wave

    start = jnp.zeros(orbitals.shape[1:], jnp.float32)
    partial_value = lax.fori_loop(0, orbitals.shape[0], accumulate, start)
    groups = lax.axis_size("band")
    summed = lax.psum(partial_value, "band")
    share = orbitals.shape[1] // groups
    mine = lax.dynamic_slice_in_dim(summed, lax.axis_index("band") * share, share, 0)
    density = mine / (orbitals.shape[0] * groups)
    source = four_pi * density
    potential = jnp.zeros_like(source)
    residual = source
    image = operate(residual)
    norm_now, product = paired_sums(residual, image)
    alpha = norm_now / product
    direction, along = (residual, image)
    for step in range(ITERS):
        potential = potential + alpha * direction
        residual = residual - alpha * along
        if step + 1 < ITERS:
            image = operate(residual)
            norm_next, product = paired_sums(residual, image)
            ratio = norm_next / norm_now
            alpha = norm_next / (product - ratio * norm_next / alpha)
            direction = residual + ratio * direction
            along = image + ratio * along
            norm_now = norm_next
    return potential


def solution(mesh):
    in_specs = (P("band", None, "space", None), P("band"))
    out_specs = P("band", "space", None)
    return jax.shard_map(local, mesh=mesh, in_specs=in_specs, out_specs=out_specs, check_vma=False)
```

profile of v0, /device:TPU:0, one launch (start us, length us, event | category | flops | bytes accessed | tf_op | source)
XLA Modules:
  0.0 320.6 jit_solution(14691085561565989361)
XLA Ops:
  6.5 30.2 %while.14 = (s32[]{:T(128)}, f32[64,40,128]{2,1,0:T(8,128)S(1)}, f32[8]{0:T(128)}, bf16[8,64,40,128]{3,2,1,0:T(8,128)(2,1)}, s32[]{:T(128)}, /*index=5*/s32[]{:T(128)}) while((s32[]{:T(128)}, f32[64,40,128]{2,1,0:T(8,128)S(1)}, f32[8]{0:T(128)}, bf16[8,64,40,128]{3,2,1,0:T(8,128)(2,1)}, s32[]{:T(128)}, /*index=5*/s32[]{:T(128)}) %tuple.46), condition=%wide.region_1.2_spmd.clone, body=%wide.region_0.1_spmd.clone.sunk | while | flops 1638403 | bytes 3276907 | solution.py:51
  6.5 1.3 dynamic_slice.31
  7.8 2.5 fusion.46
  10.3 1.3 dynamic_slice.31
  11.6 2.5 fusion.46
  14.1 1.3 dynamic_slice.31
  15.4 2.5 fusion.46
  17.9 1.3 dynamic_slice.31
  19.2 2.5 fusion.46
  21.6 1.3 dynamic_slice.31
  22.9 2.5 fusion.46
  25.4 1.3 dynamic_slice.31
  26.7 2.5 fusion.46
  29.2 1.3 dynamic_slice.31
  30.5 2.5 fusion.46
  33.0 1.3 dynamic_slice.31
  34.3 2.5 fusion.46
  37.9 86.5 %all-reduce.8.cloned.1.call-done = f32[64,40,128]{2,1,0:T(8,128)} async-done(((f32[64,40,128]{2,1,0:T(8,128)}), f32[64,40,128]{2,1,0:T(8,128)}) %all-reduce.8.cloned.1.call-update) | async-done | bytes 1310736 | tf_op jit(solution)/shard_map/psum | solution.py:53
  125.3 3.4 %collective-permute-start.1 = (f32[2,40,128]{2,1,0:T(8,128)S(1)}, f32[2,40,128]{2,1,0:T(8,128)S(1)}, u32[]{:S(2)}, u32[]{:S(2)}) collective-permute-start(f32[2,40,128]{2,1,0:T(8,128)S(1)} %get-tuple-element.138), channel_id=1, source_target_pairs={{0,4},{4,8},{8,12},{12,16},{16,20},{20,24},{24,28},{1,5},{5,9},{9,... | collective-permute-start | bytes 122888 | tf_op jit(solution)/shard_map/ppermute | solution.py:18
  130.3 4.2 %collective-permute-done = f32[2,40,128]{2,1,0:T(8,128)S(1)} collective-permute-done((f32[2,40,128]{2,1,0:T(8,128)S(1)}, f32[2,40,128]{2,1,0:T(8,128)S(1)}, u32[]{:S(2)}, u32[]{:S(2)}) %collective-permute-start) | collective-permute-done | bytes 40992 | tf_op jit(solution)/shard_map/ppermute | solution.py:19
  137.2 3.5 %collective-permute-done.2 = f32[12,2,128]{2,1,0:T(2,128)S(1)} collective-permute-done((f32[12,2,128]{2,1,0:T(2,128)S(1)}, f32[12,2,128]{2,1,0:T(2,128)S(1)}, u32[]{:S(2)}, u32[]{:S(2)}) %collective-permute-start.2) | collective-permute-done | bytes 12320 | tf_op jit(solution)/shard_map/ppermute | solution.py:19
  141.0 1.8 multiply_reduce_fusion.3
  142.8 41.2 %all-reduce.5 = (f32[]{:T(128)}, f32[]{:T(128)}) all-reduce(f32[]{:T(128)} %get-tuple-element.105, f32[]{:T(128)} %get-tuple-element.104), channel_id=1, replica_groups=mesh['band'=8,'space'=4] {'band','space'}, use_global_device_ids=true, to_apply=%region_4.5 | all-reduce | flops 2 | bytes 16 | tf_op jit(solution)/shard_map/psum | solution.py:41
  186.3 4.2 %collective-permute-start.5 = (f32[2,40,128]{2,1,0:T(8,128)S(1)}, f32[2,40,128]{2,1,0:T(8,128)S(1)}, u32[]{:S(2)}, u32[]{:S(2)}) collective-permute-start(f32[2,40,128]{2,1,0:T(8,128)S(1)} %get-tuple-element.136), channel_id=1, source_target_pairs={{0,4},{4,8},{8,12},{12,16},{16,20},{20,24},{24,28},{1,5},{5,9},{9,... | collective-permute-start | bytes 122888 | tf_op jit(solution)/shard_map/ppermute | solution.py:18
  192.1 4.2 %collective-permute-done.4 = f32[2,40,128]{2,1,0:T(8,128)S(1)} collective-permute-done((f32[2,40,128]{2,1,0:T(8,128)S(1)}, f32[2,40,128]{2,1,0:T(8,128)S(1)}, u32[]{:S(2)}, u32[]{:S(2)}) %collective-permute-start.4) | collective-permute-done | bytes 40992 | tf_op jit(solution)/shard_map/ppermute | solution.py:19
  199.0 2.8 collective-permute-done.6
  203.0 41.9 %all-reduce.4 = (f32[]{:T(128)}, f32[]{:T(128)}) all-reduce(f32[]{:T(128)} %get-tuple-element.103, f32[]{:T(128)} %get-tuple-element.102), channel_id=1, replica_groups=mesh['band'=8,'space'=4] {'band','space'}, use_global_device_ids=true, to_apply=%region_8.9 | all-reduce | flops 2 | bytes 16 | tf_op jit(solution)/shard_map/psum | solution.py:41
  249.4 4.2 %collective-permute-start.9 = (f32[2,40,128]{2,1,0:T(8,128)S(1)}, f32[2,40,128]{2,1,0:T(8,128)S(1)}, u32[]{:S(2)}, u32[]{:S(2)}) collective-permute-start(f32[2,40,128]{2,1,0:T(8,128)S(1)} %get-tuple-element.134), channel_id=1, source_target_pairs={{0,4},{4,8},{8,12},{12,16},{16,20},{20,24},{24,28},{1,5},{5,9},{9,... | collective-permute-start | bytes 122888 | tf_op jit(solution)/shard_map/ppermute | solution.py:18
  255.2 4.2 %collective-permute-done.8 = f32[2,40,128]{2,1,0:T(8,128)S(1)} collective-permute-done((f32[2,40,128]{2,1,0:T(8,128)S(1)}, f32[2,40,128]{2,1,0:T(8,128)S(1)}, u32[]{:S(2)}, u32[]{:S(2)}) %collective-permute-start.8) | collective-permute-done | bytes 40992 | tf_op jit(solution)/shard_map/ppermute | solution.py:19
  262.1 3.1 collective-permute-done.10
  266.5 41.9 %all-reduce.3 = (f32[]{:T(128)}, f32[]{:T(128)}) all-reduce(f32[]{:T(128)} %get-tuple-element.101, f32[]{:T(128)} %get-tuple-element.100), channel_id=1, replica_groups=mesh['band'=8,'space'=4] {'band','space'}, use_global_device_ids=true, to_apply=%region_12.13 | all-reduce | flops 2 | bytes 16 | tf_op jit(solution)/shard_map/psum | solution.py:41
  312.1 1.6 multiply_add_fusion
  (37 shorter events, 18.5 us)
Async XLA Ops:
  6.5 117.8 %all-reduce.8.cloned.1.call-start = ((), (), s32[]{:S(2)}) async-start(), calls=%async_computation | async-start | bytes 2621440 | tf_op jit(solution)/shard_map/psum | solution.py:53
  36.7 1.1 copy-start
  125.3 5.0 %collective-permute-start.1 = (f32[2,40,128]{2,1,0:T(8,128)S(1)}, f32[2,40,128]{2,1,0:T(8,128)S(1)}, u32[]{:S(2)}, u32[]{:S(2)}) collective-permute-start(f32[2,40,128]{2,1,0:T(8,128)S(1)} %get-tuple-element.138), channel_id=1, source_target_pairs={{0,4},{4,8},{8,12},{12,16},{16,20},{20,24},{24,28},{1,5},{5,9},{9,... | collective-permute-start | bytes 122888 | tf_op jit(solution)/shard_map/ppermute | solution.py:18
  128.7 5.9 %collective-permute-start = (f32[2,40,128]{2,1,0:T(8,128)S(1)}, f32[2,40,128]{2,1,0:T(8,128)S(1)}, u32[]{:S(2)}, u32[]{:S(2)}) collective-permute-start(f32[2,40,128]{2,1,0:T(8,128)S(1)} %get-tuple-element.139), channel_id=1, source_target_pairs={{4,0},{8,4},{12,8},{16,12},{20,16},{24,20},{28,24},{5,1},{9,5},{13... | collective-permute-start | bytes 122888 | tf_op jit(solution)/shard_map/ppermute | solution.py:19
  134.6 2.6 collective-permute-start.3
  135.9 4.8 %collective-permute-start.2 = (f32[12,2,128]{2,1,0:T(2,128)S(1)}, f32[12,2,128]{2,1,0:T(2,128)S(1)}, u32[]{:S(2)}, u32[]{:S(2)}) collective-permute-start(f32[12,2,128]{2,1,0:T(2,128)S(1)} %get-tuple-element.133), channel_id=1, source_target_pairs={{1,0},{2,1},{3,2},{5,4},{6,5},{7,6},{9,8},{10,9},{11,10},{13,12},{... | collective-permute-start | bytes 36872 | tf_op jit(solution)/shard_map/ppermute | solution.py:19
  186.3 5.8 %collective-permute-start.5 = (f32[2,40,128]{2,1,0:T(8,128)S(1)}, f32[2,40,128]{2,1,0:T(8,128)S(1)}, u32[]{:S(2)}, u32[]{:S(2)}) collective-permute-start(f32[2,40,128]{2,1,0:T(8,128)S(1)} %get-tuple-element.136), channel_id=1, source_target_pairs={{0,4},{4,8},{8,12},{12,16},{16,20},{20,24},{24,28},{1,5},{5,9},{9,... | collective-permute-start | bytes 122888 | tf_op jit(solution)/shard_map/ppermute | solution.py:18
  190.5 5.9 %collective-permute-start.4 = (f32[2,40,128]{2,1,0:T(8,128)S(1)}, f32[2,40,128]{2,1,0:T(8,128)S(1)}, u32[]{:S(2)}, u32[]{:S(2)}) collective-permute-start(f32[2,40,128]{2,1,0:T(8,128)S(1)} %get-tuple-element.137), channel_id=1, source_target_pairs={{4,0},{8,4},{12,8},{16,12},{20,16},{24,20},{28,24},{5,1},{9,5},{13... | collective-permute-start | bytes 122888 | tf_op jit(solution)/shard_map/ppermute | solution.py:19
  196.4 2.6 collective-permute-start.7
  197.7 4.1 %collective-permute-start.6 = (f32[12,2,128]{2,1,0:T(2,128)S(1)}, f32[12,2,128]{2,1,0:T(2,128)S(1)}, u32[]{:S(2)}, u32[]{:S(2)}) collective-permute-start(f32[12,2,128]{2,1,0:T(2,128)S(1)} %get-tuple-element.129), channel_id=1, source_target_pairs={{1,0},{2,1},{3,2},{5,4},{6,5},{7,6},{9,8},{10,9},{11,10},{13,12},{... | collective-permute-start | bytes 36872 | tf_op jit(solution)/shard_map/ppermute | solution.py:19
  249.4 5.8 %collective-permute-start.9 = (f32[2,40,128]{2,1,0:T(8,128)S(1)}, f32[2,40,128]{2,1,0:T(8,128)S(1)}, u32[]{:S(2)}, u32[]{:S(2)}) collective-permute-start(f32[2,40,128]{2,1,0:T(8,128)S(1)} %get-tuple-element.134), channel_id=1, source_target_pairs={{0,4},{4,8},{8,12},{12,16},{16,20},{20,24},{24,28},{1,5},{5,9},{9,... | collective-permute-start | bytes 122888 | tf_op jit(solution)/shard_map/ppermute | solution.py:18
  253.6 5.9 %collective-permute-start.8 = (f32[2,40,128]{2,1,0:T(8,128)S(1)}, f32[2,40,128]{2,1,0:T(8,128)S(1)}, u32[]{:S(2)}, u32[]{:S(2)}) collective-permute-start(f32[2,40,128]{2,1,0:T(8,128)S(1)} %get-tuple-element.135), channel_id=1, source_target_pairs={{4,0},{8,4},{12,8},{16,12},{20,16},{24,20},{28,24},{5,1},{9,5},{13... | collective-permute-start | bytes 122888 | tf_op jit(solution)/shard_map/ppermute | solution.py:19
  259.5 2.6 collective-permute-start.11
  260.8 4.4 %collective-permute-start.10 = (f32[12,2,128]{2,1,0:T(2,128)S(1)}, f32[12,2,128]{2,1,0:T(2,128)S(1)}, u32[]{:S(2)}, u32[]{:S(2)}) collective-permute-start(f32[12,2,128]{2,1,0:T(2,128)S(1)} %get-tuple-element.125), channel_id=1, source_target_pairs={{1,0},{2,1},{3,2},{5,4},{6,5},{7,6},{9,8},{10,9},{11,10},{13,12},{... | collective-permute-start | bytes 36872 | tf_op jit(solution)/shard_map/ppermute | solution.py:19
Sparse Core Ops, SparseCore 0:
  38.0 86.3 all-reduce.7
where the time goes:
time: 322 us; the launch traced here: 321 us
  blocking collectives  125 us (39%)
  waiting for transfers between devices  110 us (34%)
  other arithmetic  27.8 us (9%)
  starting transfers between devices  23.4 us (7%)
  between operations  23 us (7%)
  local copies, waits for them, and re-layouts  11.5 us (4%)
    psum x3, blocking collectives, paired_sums(): lax.psum((jnp.sum(residual * residual), jnp.sum(residual * image)), ('ban...  125 us
    psum x1, waiting for transfers between devices, local(): summed = lax.psum(partial_value, 'band')  86.5 us
    ppermute x6, waiting for transfers between devices, with_halo(): after = lax.ppermute(first, axis, down)  22.1 us
    add x8, other arithmetic, accumulate(): return total + occupations[index] * wave * wave  19.6 us
    ppermute x6, starting transfers between devices, with_halo(): before = lax.ppermute(last, axis, up)  15.6 us
    dynamic_slice x8, local copies, waits for them, and re-layouts, accumulate(): return total + occupations[index] * wave * wave  10.4 us
    ppermute x6, starting transfers between devices, with_halo(): after = lax.ppermute(first, axis, down)  7.75 us
  transfers between devices with their start and end apart: 13, of which 10 were waited for; matrix products, arithmetic and copies ran while one was open for 0% of the time, Pallas kernels for 0%

commit v1 on v0

--- a/solution.py
+++ b/solution.py
@@ -6,6 +6,15 @@
 
 ITERS = 3
 four_pi = 4.0 * math.pi
+
+
+def edit_samples(my_data):
+    devs = lax.axis_size("band")
+    carry_in = my_data
+    for idx in [[(jj, jj ^ q) for jj in range(devs)] for q in (1, 2, 4, 8, 16) if q < devs]:
+        local_now = lax.ppermute(carry_in, axis_name="band", perm=idx)
+        carry_in = carry_in + local_now
+    return carry_in
 
 
 def with_halo(shard, sides, width):
@@ -50,7 +59,7 @@
     start = jnp.zeros(orbitals.shape[1:], jnp.float32)
     partial_value = lax.fori_loop(0, orbitals.shape[0], accumulate, start)
     groups = lax.axis_size("band")
-    summed = lax.psum(partial_value, "band")
+    summed = edit_samples(partial_value)
     share = orbitals.shape[1] // groups
     mine = lax.dynamic_slice_in_dim(summed, lax.axis_index("band") * share, share, 0)
     density = mine / (orbitals.shape[0] * groups)

time: 322 us -> 336 us (1.043)
  starting transfers between devices: 23.4 us -> 36.8 us
  between operations: 23 us -> 9.76 us
  waiting for transfers between devices: 110 us -> 123 us
  blocking collectives: 125 us -> 131 us
  other arithmetic: 27.8 us -> 23.8 us
    ppermute x0 -> x3, waiting for transfers between devices: none -> 112 us  [edit_samples(): local_now = lax.ppermute(carry_in, axis_name='band', perm=idx)]
    psum x1 -> x0, waiting for transfers between devices: 86.5 us -> none  [local(): summed = lax.psum(partial_value, 'band')]
    ppermute x6, waiting for transfers between devices: 22.1 us -> 4.32 us  [with_halo(): after = lax.ppermute(first, axis, down)]
    ppermute x0 -> x3, starting transfers between devices: none -> 7.55 us  [edit_samples(): local_now = lax.ppermute(carry_in, axis_name='band', perm=idx)]
    ppermute x6, starting transfers between devices: 15.6 us -> 21.5 us  [with_halo(): before = lax.ppermute(last, axis, up)]
    psum x3, blocking collectives: 125 us -> 131 us  [paired_sums(): lax.psum((jnp.sum(residual * residual), jnp.sum(residual * image)), ('ban...]
    ppermute x6, waiting for transfers between devices: 1.07 us -> 6.46 us  [with_halo(): before = lax.ppermute(last, axis, up)]
  transfers between devices with their start and end apart: 13 -> 15, of which waited for: 10 -> 9; matrix products, arithmetic and copies ran while one was open for 0% -> 0% of each run, Pallas kernels for 0% -> 0%
where the time goes in v1:
time: 336 us; the launch traced here: 334 us
  blocking collectives  131 us (39%)
  waiting for transfers between devices  123 us (37%)
  starting transfers between devices  36.8 us (11%)
  other arithmetic  23.8 us (7%)
  local copies, waits for them, and re-layouts  9.9 us (3%)
  between operations  9.76 us (3%)
    psum x3, blocking collectives, paired_sums(): lax.psum((jnp.sum(residual * residual), jnp.sum(residual * image)), ('ban...  131 us
    ppermute x3, waiting for transfers between devices, edit_samples(): local_now = lax.ppermute(carry_in, axis_name='band', perm=idx)  112 us
    ppermute x6, starting transfers between devices, with_halo(): before = lax.ppermute(last, axis, up)  21.5 us
    add x8, other arithmetic, accumulate(): return total + occupations[index] * wave * wave  19 us
    dynamic_slice x8, local copies, waits for them, and re-layouts, accumulate(): return total + occupations[index] * wave * wave  9.87 us
    ppermute x6, starting transfers between devices, with_halo(): after = lax.ppermute(first, axis, down)  7.75 us
    ppermute x3, starting transfers between devices, edit_samples(): local_now = lax.ppermute(carry_in, axis_name='band', perm=idx)  7.55 us
  transfers between devices with their start and end apart: 15, of which 9 were waited for; matrix products, arithmetic and copies ran while one was open for 0% of the time, Pallas kernels for 0%

profile of v1, /device:TPU:0, one launch (start us, length us, event | category | flops | bytes accessed | tf_op | source)
XLA Modules:
  0.0 334.3 jit_solution(8773211969972731633)
XLA Ops:
  0.0 29.0 %while.14 = (s32[]{:T(128)}, f32[64,40,128]{2,1,0:T(8,128)S(1)}, f32[8]{0:T(128)}, bf16[8,64,40,128]{3,2,1,0:T(8,128)(2,1)}, s32[]{:T(128)}, /*index=5*/s32[]{:T(128)}) while((s32[]{:T(128)}, f32[64,40,128]{2,1,0:T(8,128)S(1)}, f32[8]{0:T(128)}, bf16[8,64,40,128]{3,2,1,0:T(8,128)(2,1)}, s32[]{:T(128)}, /*index=5*/s32[]{:T(128)}) %tuple.47), condition=%wide.region_1.2_spmd.clone, body=%wide.region_0.1_spmd.clone.sunk | while | flops 1638403 | bytes 3276899 | solution.py:60
  1.2 2.4 fusion.46
  4.9 2.4 fusion.46
  8.5 2.4 fusion.46
  12.1 2.4 fusion.46
  15.8 2.4 fusion.46
  19.4 2.4 fusion.46
  23.0 2.4 fusion.46
  26.7 2.4 fusion.46
  29.0 3.0 collective-permute-start
  32.1 28.8 %collective-permute-done = f32[64,40,128]{2,1,0:T(8,128)S(1)} collective-permute-done((f32[64,40,128]{2,1,0:T(8,128)S(1)}, f32[64,40,128]{2,1,0:T(8,128)S(1)}, u32[]{:S(2)}, u32[]{:S(2)}) %collective-permute-start) | collective-permute-done | bytes 1310752 | tf_op jit(solution)/shard_map/ppermute | solution.py:15
  61.0 1.9 collective-permute-start.1
  62.9 28.1 %collective-permute-done.1 = f32[64,40,128]{2,1,0:T(8,128)S(1)} collective-permute-done((f32[64,40,128]{2,1,0:T(8,128)S(1)}, f32[64,40,128]{2,1,0:T(8,128)S(1)}, u32[]{:S(2)}, u32[]{:S(2)}) %collective-permute-start.1) | collective-permute-done | bytes 1310752 | tf_op jit(solution)/shard_map/ppermute | solution.py:15
  91.1 2.6 collective-permute-start.2
  93.8 55.5 %collective-permute-done.2 = f32[64,40,128]{2,1,0:T(8,128)S(1)} collective-permute-done((f32[64,40,128]{2,1,0:T(8,128)S(1)}, f32[64,40,128]{2,1,0:T(8,128)S(1)}, u32[]{:S(2)}, u32[]{:S(2)}) %collective-permute-start.2) | collective-permute-done | bytes 1310752 | tf_op jit(solution)/shard_map/ppermute | solution.py:15
  149.3 1.3 collective-permute-start.3
  150.6 4.5 %collective-permute-start.4 = (f32[2,40,128]{2,1,0:T(8,128)S(1)}, f32[2,40,128]{2,1,0:T(8,128)S(1)}, u32[]{:S(2)}, u32[]{:S(2)}) collective-permute-start(f32[2,40,128]{2,1,0:T(8,128)S(1)} %get-tuple-element.140), channel_id=1, source_target_pairs={{0,4},{4,8},{8,12},{12,16},{16,20},{20,24},{24,28},{1,5},{5,9},{9,... | collective-permute-start | bytes 122888 | tf_op jit(solution)/shard_map/ppermute | solution.py:27
  155.2 1.6 collective-permute-done.4
  156.8 1.3 collective-permute-start.5
  158.1 3.0 collective-permute-start.6
  163.3 43.2 %all-reduce.5 = (f32[]{:T(128)}, f32[]{:T(128)}) all-reduce(f32[]{:T(128)} %get-tuple-element.105, f32[]{:T(128)} %get-tuple-element.104), channel_id=1, replica_groups=mesh['band'=8,'space'=4] {'band','space'}, use_global_device_ids=true, to_apply=%region_3.4 | all-reduce | flops 2 | bytes 16 | tf_op jit(solution)/shard_map/psum | solution.py:50
  207.7 1.3 collective-permute-start.7
  209.0 4.8 %collective-permute-start.8 = (f32[2,40,128]{2,1,0:T(8,128)S(1)}, f32[2,40,128]{2,1,0:T(8,128)S(1)}, u32[]{:S(2)}, u32[]{:S(2)}) collective-permute-start(f32[2,40,128]{2,1,0:T(8,128)S(1)} %get-tuple-element.138), channel_id=1, source_target_pairs={{0,4},{4,8},{8,12},{12,16},{16,20},{20,24},{24,28},{1,5},{5,9},{9,... | collective-permute-start | bytes 122888 | tf_op jit(solution)/shard_map/ppermute | solution.py:27
  213.9 1.6 collective-permute-done.8
  216.8 1.3 collective-permute-start.9
  218.1 4.2 %collective-permute-done.9 = f32[12,2,128]{2,1,0:T(2,128)S(1)} collective-permute-done((f32[12,2,128]{2,1,0:T(2,128)S(1)}, f32[12,2,128]{2,1,0:T(2,128)S(1)}, u32[]{:S(2)}, u32[]{:S(2)}) %collective-permute-start.9) | collective-permute-done | bytes 12320 | tf_op jit(solution)/shard_map/ppermute | solution.py:28
  223.6 43.0 %all-reduce.4 = (f32[]{:T(128)}, f32[]{:T(128)}) all-reduce(f32[]{:T(128)} %get-tuple-element.103, f32[]{:T(128)} %get-tuple-element.102), channel_id=1, replica_groups=mesh['band'=8,'space'=4] {'band','space'}, use_global_device_ids=true, to_apply=%region_7.8 | all-reduce | flops 2 | bytes 16 | tf_op jit(solution)/shard_map/psum | solution.py:50
  272.4 4.8 %collective-permute-start.12 = (f32[2,40,128]{2,1,0:T(8,128)S(1)}, f32[2,40,128]{2,1,0:T(8,128)S(1)}, u32[]{:S(2)}, u32[]{:S(2)}) collective-permute-start(f32[2,40,128]{2,1,0:T(8,128)S(1)} %get-tuple-element.136), channel_id=1, source_target_pairs={{0,4},{4,8},{8,12},{12,16},{16,20},{20,24},{24,28},{1,5},{5,9},{9,... | collective-permute-start | bytes 122888 | tf_op jit(solution)/shard_map/ppermute | solution.py:27
  277.2 1.6 collective-permute-done.12
  278.8 1.3 collective-permute-start.13
  280.1 3.0 collective-permute-start.14
  285.2 44.6 %all-reduce.3 = (f32[]{:T(128)}, f32[]{:T(128)}) all-reduce(f32[]{:T(128)} %get-tuple-element.101, f32[]{:T(128)} %get-tuple-element.100), channel_id=1, replica_groups=mesh['band'=8,'space'=4] {'band','space'}, use_global_device_ids=true, to_apply=%region_11.12 | all-reduce | flops 2 | bytes 16 | tf_op jit(solution)/shard_map/psum | solution.py:50
  (40 shorter events, 19.0 us)
Async XLA Ops:
  29.0 31.8 %collective-permute-start = (f32[64,40,128]{2,1,0:T(8,128)S(1)}, f32[64,40,128]{2,1,0:T(8,128)S(1)}, u32[]{:S(2)}, u32[]{:S(2)}) collective-permute-start(f32[64,40,128]{2,1,0:T(8,128)S(1)} %get-tuple-element.84), channel_id=1, source_target_pairs={{0,4},{4,0},{8,12},{12,8},{16,20},{20,16},{24,28},{28,24},{1,5},{5... | collective-permute-start | bytes 3932168 | tf_op jit(solution)/shard_map/ppermute | solution.py:15
  61.0 30.0 %collective-permute-start.1 = (f32[64,40,128]{2,1,0:T(8,128)S(1)}, f32[64,40,128]{2,1,0:T(8,128)S(1)}, u32[]{:S(2)}, u32[]{:S(2)}) collective-permute-start(f32[64,40,128]{2,1,0:T(8,128)S(1)} %add.174), channel_id=1, source_target_pairs={{0,8},{4,12},{8,0},{12,4},{16,24},{20,28},{24,16},{28,20},{1,9},{5... | collective-permute-start | bytes 3932168 | tf_op jit(solution)/shard_map/ppermute | solution.py:15
  91.1 58.1 %collective-permute-start.2 = (f32[64,40,128]{2,1,0:T(8,128)S(1)}, f32[64,40,128]{2,1,0:T(8,128)S(1)}, u32[]{:S(2)}, u32[]{:S(2)}) collective-permute-start(f32[64,40,128]{2,1,0:T(8,128)S(1)} %add.175), channel_id=1, source_target_pairs={{0,16},{4,20},{8,24},{12,28},{16,0},{20,4},{24,8},{28,12},{1,17},{... | collective-permute-start | bytes 3932168 | tf_op jit(solution)/shard_map/ppermute | solution.py:15
  149.3 5.9 %collective-permute-start.3 = (f32[2,40,128]{2,1,0:T(8,128)S(1)}, f32[2,40,128]{2,1,0:T(8,128)S(1)}, u32[]{:S(2)}, u32[]{:S(2)}) collective-permute-start(f32[2,40,128]{2,1,0:T(8,128)S(1)} %get-tuple-element.141), channel_id=1, source_target_pairs={{4,0},{8,4},{12,8},{16,12},{20,16},{24,20},{28,24},{5,1},{9,5},{13... | collective-permute-start | bytes 122888 | tf_op jit(solution)/shard_map/ppermute | solution.py:28
  150.6 6.2 %collective-permute-start.4 = (f32[2,40,128]{2,1,0:T(8,128)S(1)}, f32[2,40,128]{2,1,0:T(8,128)S(1)}, u32[]{:S(2)}, u32[]{:S(2)}) collective-permute-start(f32[2,40,128]{2,1,0:T(8,128)S(1)} %get-tuple-element.140), channel_id=1, source_target_pairs={{0,4},{4,8},{8,12},{12,16},{16,20},{20,24},{24,28},{1,5},{5,9},{9,... | collective-permute-start | bytes 122888 | tf_op jit(solution)/shard_map/ppermute | solution.py:27
  156.8 4.3 %collective-permute-start.5 = (f32[12,2,128]{2,1,0:T(2,128)S(1)}, f32[12,2,128]{2,1,0:T(2,128)S(1)}, u32[]{:S(2)}, u32[]{:S(2)}) collective-permute-start(f32[12,2,128]{2,1,0:T(2,128)S(1)} %get-tuple-element.135), channel_id=1, source_target_pairs={{1,0},{2,1},{3,2},{5,4},{6,5},{7,6},{9,8},{10,9},{11,10},{13,12},{... | collective-permute-start | bytes 36872 | tf_op jit(solution)/shard_map/ppermute | solution.py:28
  158.1 3.9 %collective-permute-start.6 = (f32[12,2,128]{2,1,0:T(2,128)S(1)}, f32[12,2,128]{2,1,0:T(2,128)S(1)}, u32[]{:S(2)}, u32[]{:S(2)}) collective-permute-start(f32[12,2,128]{2,1,0:T(2,128)S(1)} %get-tuple-element.134), channel_id=1, source_target_pairs={{0,1},{1,2},{2,3},{4,5},{5,6},{6,7},{8,9},{9,10},{10,11},{12,13},{... | collective-permute-start | bytes 36872 | tf_op jit(solution)/shard_map/ppermute | solution.py:27
  207.7 6.2 %collective-permute-start.7 = (f32[2,40,128]{2,1,0:T(8,128)S(1)}, f32[2,40,128]{2,1,0:T(8,128)S(1)}, u32[]{:S(2)}, u32[]{:S(2)}) collective-permute-start(f32[2,40,128]{2,1,0:T(8,128)S(1)} %get-tuple-element.139), channel_id=1, source_target_pairs={{4,0},{8,4},{12,8},{16,12},{20,16},{24,20},{28,24},{5,1},{9,5},{13... | collective-permute-start | bytes 122888 | tf_op jit(solution)/shard_map/ppermute | solution.py:28
  209.0 6.5 %collective-permute-start.8 = (f32[2,40,128]{2,1,0:T(8,128)S(1)}, f32[2,40,128]{2,1,0:T(8,128)S(1)}, u32[]{:S(2)}, u32[]{:S(2)}) collective-permute-start(f32[2,40,128]{2,1,0:T(8,128)S(1)} %get-tuple-element.138), channel_id=1, source_target_pairs={{0,4},{4,8},{8,12},{12,16},{16,20},{20,24},{24,28},{1,5},{5,9},{9,... | collective-permute-start | bytes 122888 | tf_op jit(solution)/shard_map/ppermute | solution.py:27
  215.5 2.6 collective-permute-start.10
  216.8 5.5 %collective-permute-start.9 = (f32[12,2,128]{2,1,0:T(2,128)S(1)}, f32[12,2,128]{2,1,0:T(2,128)S(1)}, u32[]{:S(2)}, u32[]{:S(2)}) collective-permute-start(f32[12,2,128]{2,1,0:T(2,128)S(1)} %get-tuple-element.131), channel_id=1, source_target_pairs={{1,0},{2,1},{3,2},{5,4},{6,5},{7,6},{9,8},{10,9},{11,10},{13,12},{... | collective-permute-start | bytes 36872 | tf_op jit(solution)/shard_map/ppermute | solution.py:28
  271.1 6.2 %collective-permute-start.11 = (f32[2,40,128]{2,1,0:T(8,128)S(1)}, f32[2,40,128]{2,1,0:T(8,128)S(1)}, u32[]{:S(2)}, u32[]{:S(2)}) collective-permute-start(f32[2,40,128]{2,1,0:T(8,128)S(1)} %get-tuple-element.137), channel_id=1, source_target_pairs={{4,0},{8,4},{12,8},{16,12},{20,16},{24,20},{28,24},{5,1},{9,5},{13... | collective-permute-start | bytes 122888 | tf_op jit(solution)/shard_map/ppermute | solution.py:28
  272.4 6.5 %collective-permute-start.12 = (f32[2,40,128]{2,1,0:T(8,128)S(1)}, f32[2,40,128]{2,1,0:T(8,128)S(1)}, u32[]{:S(2)}, u32[]{:S(2)}) collective-permute-start(f32[2,40,128]{2,1,0:T(8,128)S(1)} %get-tuple-element.136), channel_id=1, source_target_pairs={{0,4},{4,8},{8,12},{12,16},{16,20},{20,24},{24,28},{1,5},{5,9},{9,... | collective-permute-start | bytes 122888 | tf_op jit(solution)/shard_map/ppermute | solution.py:27
  278.8 4.3 %collective-permute-start.13 = (f32[12,2,128]{2,1,0:T(2,128)S(1)}, f32[12,2,128]{2,1,0:T(2,128)S(1)}, u32[]{:S(2)}, u32[]{:S(2)}) collective-permute-start(f32[12,2,128]{2,1,0:T(2,128)S(1)} %get-tuple-element.127), channel_id=1, source_target_pairs={{1,0},{2,1},{3,2},{5,4},{6,5},{7,6},{9,8},{10,9},{11,10},{13,12},{... | collective-permute-start | bytes 36872 | tf_op jit(solution)/shard_map/ppermute | solution.py:28
  280.1 3.9 %collective-permute-start.14 = (f32[12,2,128]{2,1,0:T(2,128)S(1)}, f32[12,2,128]{2,1,0:T(2,128)S(1)}, u32[]{:S(2)}, u32[]{:S(2)}) collective-permute-start(f32[12,2,128]{2,1,0:T(2,128)S(1)} %get-tuple-element.126), channel_id=1, source_target_pairs={{0,1},{1,2},{2,3},{4,5},{5,6},{6,7},{8,9},{9,10},{10,11},{12,13},{... | collective-permute-start | bytes 36872 | tf_op jit(solution)/shard_map/ppermute | solution.py:27
